TPU v7x, 32 devices: a whole 2x2x4 slice. The times are simulated.
32 devices in a mesh: pr: 8 (over y, x, core), pc: 4 (over z).
Axes of the slice: x: 2, y: 2, z: 4, core: 2. Of those that a mesh axis runs over, the one named last changes fastest.
Arguments:
- pair_array: bfloat16 [256, 256, 128], P('pr', 'pc'), may hold values from -6 to 6
- left_weight: bfloat16 [128, 128], replicated, may hold values from -0.5 to 0.5
- right_weight: bfloat16 [128, 128], replicated, may hold values from -0.5 to 0.5
- left_gate: bfloat16 [128, 128], replicated, may hold values from -0.5 to 0.5
- right_gate: bfloat16 [128, 128], replicated, may hold values from -0.5 to 0.5
- mid_gain: float32 [128], replicated, may hold values from 0.25 to 1.75
- out_weight: bfloat16 [128, 128], replicated, may hold values from -0.5 to 0.5
- out_gate: bfloat16 [128, 128], replicated, may hold values from -0.5 to 0.5
Outputs:
- pair_update: bfloat16 [256, 256, 128], P('pr', 'pc')
All inputs are finite; a program needn't handle non-finite values.
Results may differ from a plain program's by a relative error of at most 0.012.
Values may be sent and summed in bfloat16 or wider, within the bound.
No kernel may reach another device: no remote copies, remote signals or barrier semaphores. Data moves between devices by JAX's collectives and lax.ppermute only.
A program may use at most 128 MiB of HBM per device.

v0:
```python
import jax
import jax.numpy as jnp
from jax import lax
from jax.sharding import PartitionSpec as P


def unit_channels(values, channel_gain):
    centred = values - jnp.mean(values, axis=-1, keepdims=True)
    return (
        centred
        * lax.rsqrt(jnp.mean(centred * centred, axis=-1, keepdims=True) + 1e-05)
        * channel_gain
    )


def make_factors(pair_in, left_weight, right_weight, left_gate, right_gate):
    left = jnp.einsum("ijc,cd->ijd", pair_in, left_weight, preferred_element_type=jnp.float32)
    left = left * jax.nn.sigmoid(
        jnp.einsum("ijc,cd->ijd", pair_in, left_gate, preferred_element_type=jnp.float32)
    )
    right = jnp.einsum("ijc,cd->ijd", pair_in, right_weight, preferred_element_type=jnp.float32)
    right = right * jax.nn.sigmoid(
        jnp.einsum("ijc,cd->ijd", pair_in, right_gate, preferred_element_type=jnp.float32)
    )
    return (pair_in, left.astype(jnp.bfloat16), right.astype(jnp.bfloat16))


def to_pair(mixed, ready, mid_gain, out_weight, out_gate):
    scaled = unit_channels(mixed.astype(jnp.float32), mid_gain).astype(jnp.bfloat16)
    scaled = lax.optimization_barrier(scaled)
    gate = jax.nn.sigmoid(
        jnp.einsum("ijc,cd->ijd", ready, out_gate, preferred_element_type=jnp.float32)
    )
    return (
        jnp.einsum("ijd,dc->ijc", scaled, out_weight, preferred_element_type=jnp.float32) * gate
    ).astype(jnp.bfloat16)


def on_device(
    pair_array, left_weight, right_weight, left_gate, right_gate, mid_gain, out_weight, out_gate
):
    ready, left, right = make_factors(pair_array, left_weight, right_weight, left_gate, right_gate)
    count = pair_array.shape[0] * lax.axis_size("pr")
    left_lines, right_lines = (
        lax.all_to_all(left, "pr", split_axis=2, concat_axis=0, tiled=True),
        lax.all_to_all(right, "pr", split_axis=2, concat_axis=0, tiled=True),
    )
    strip = jnp.einsum(
        "kid,kjd->ijd",
        lax.all_gather(left_lines, "pc", axis=1, tiled=True),
        right_lines,
        preferred_element_type=jnp.float32,
    )
    strip = (strip * count ** (-0.5)).astype(jnp.bfloat16)
    mixed = lax.all_to_all(strip, "pr", split_axis=0, concat_axis=2, tiled=True)
    return to_pair(mixed, ready, mid_gain, out_weight, out_gate)


def solution(mesh):
    return jax.shard_map(
        on_device,
        mesh=mesh,
        in_specs=(P("pr", "pc", None), P(), P(), P(), P(), P(), P(), P()),
        out_specs=P("pr", "pc", None),
        check_vma=False,
    )
```

profile of v0, /device:TPU:0, one launch (start us, length us, event | category | flops | bytes accessed | tf_op | source)
XLA Modules:
  0.0 104.0 jit_solution(1541400130074911763)
XLA Ops:
  6.5 1.0 copy-done
  7.6 1.0 fusion.24
  8.6 1.2 %fusion.14 = bf16[32,64,128]{2,1,0:T(8,128)(2,1)S(1)} fusion(f32[32,64,128]{2,1,0:T(8,128)S(1)} %fusion.24, bf16[32,64,128]{2,1,0:T(8,128)(2,1)S(1)} %copy-done, bf16[128,128]{1,0:T(8,128)(2,1)} %param.11), kind=kOutput, calls=%fused_computation.22 | convolution fusion | flops 68419584 | bytes 2129920 | tf_op jit(solution)/shard_map/ijc,cd->ijd/dot_general | solution.py:19
  9.8 1.6 %copy.25 = bf16[32,64,128]{1,0,2:T(8,128)(2,1)S(1)} copy(bf16[32,64,128]{2,1,0:T(8,128)(2,1)S(1)} %fusion.14) | data formatting | bytes 1048576 | tf_op jit(solution)/shard_map/convert_element_type | solution.py:25
  11.4 0.7 reshape.28
  12.2 14.7 %all_to_all.45 = bf16[8,2,16384]{2,1,0:T(2,128)(2,1)S(1)} all-to-all(bf16[8,2,16384]{2,1,0:T(2,128)(2,1)S(1)} %reshape.28), channel_id=1, replica_groups=mesh['pr'=8,'pc'=4] {'pr'}, dimensions={0} | all-to-all | bytes 1048576 | tf_op jit(solution)/shard_map/all_to_all | solution.py:45
  26.8 0.7 reshape.29
  27.5 0.4 copy.27
  28.0 1.6 %copy.28 = bf16[256,64,16]{0,1,2:T(8,128)(2,1)} copy(bf16[256,64,16]{1,2,0:T(8,128)(2,1)S(1)} %bitcast.66) | data formatting | bytes 1048576 | tf_op jit(solution)/shard_map/all_to_all | solution.py:45
  29.9 0.4 fusion.15
  30.4 1.6 %copy.22 = bf16[32,64,128]{1,0,2:T(8,128)(2,1)S(1)} copy(bf16[32,64,128]{2,1,0:T(8,128)(2,1)S(1)} %fusion.15) | data formatting | bytes 1048576 | tf_op jit(solution)/shard_map/convert_element_type | solution.py:25
  32.0 0.7 reshape.30
  32.7 12.1 %all_to_all.46 = bf16[8,2,16384]{2,1,0:T(2,128)(2,1)S(1)} all-to-all(bf16[8,2,16384]{2,1,0:T(2,128)(2,1)S(1)} %reshape.30), channel_id=1, replica_groups=mesh['pr'=8,'pc'=4] {'pr'}, dimensions={0} | all-to-all | bytes 1048576 | tf_op jit(solution)/shard_map/all_to_all | solution.py:46
  44.8 0.7 reshape.31
  45.9 28.9 %all-gather.2.cloned.1.call-done = bf16[256,256,16]{0,1,2:T(8,128)(2,1)} async-done(((bf16[256,64,16]{0,1,2:T(8,128)(2,1)}), bf16[256,256,16]{0,1,2:T(8,128)(2,1)}) %all-gather.2.cloned.1.call-update) | async-done | bytes 2097168 | tf_op jit(solution)/shard_map/all_gather | solution.py:50
  74.8 2.4 %fusion.18 = bf16[256,64,16]{0,1,2:T(8,128)(2,1)S(1)} fusion(bf16[256,256,16]{0,1,2:T(8,128)(2,1)} %all-gather.2.cloned.1.call-done, bf16[256,64,16]{1,2,0:T(8,128)(2,1)S(1)} %bitcast.61), kind=kOutput, calls=%fused_computation.26 | convolution fusion | flops 134742016 | bytes 3145728 | tf_op jit(solution)/shard_map/kid,kjd->ijd/dot_general | solution.py:48
  77.2 1.0 copy.30
  78.1 1.5 %reshape.32 = bf16[8,2,16384]{2,1,0:T(2,128)(2,1)} reshape(bf16[256,16,64]{2,1,0:T(8,128)(2,1)S(1)} %bitcast.64) | data formatting | bytes 1048576
  79.6 3.7 %all-to-all-start.2 = ((bf16[8,2,16384]{2,1,0:T(2,128)(2,1)}), bf16[8,2,16384]{2,1,0:T(2,128)(2,1)S(1)}, u32[]{:S(2)}, u32[]{:S(2)}) async-start(bf16[8,2,16384]{2,1,0:T(2,128)(2,1)} %reshape.32), calls=%async_computation.2 | async-start | bytes 1048576 | tf_op jit(solution)/shard_map/all_to_all | solution.py:55
  83.3 0.4 fusion.13
  83.8 9.3 %all-to-all-done.2 = bf16[8,2,16384]{2,1,0:T(2,128)(2,1)S(1)} async-done(((bf16[8,2,16384]{2,1,0:T(2,128)(2,1)}), bf16[8,2,16384]{2,1,0:T(2,128)(2,1)S(1)}, u32[]{:S(2)}, u32[]{:S(2)}) %all-to-all-start.2) | async-done | bytes 524320 | tf_op jit(solution)/shard_map/all_to_all | solution.py:55
  93.0 0.7 reshape.33
  95.2 0.5 fusion.2
  95.9 1.3 %fusion.17 = bf16[32,64,128]{2,1,0:T(8,128)(2,1)} fusion(f32[32,64,128]{2,1,0:T(8,128)S(1)} %fusion.13, bf16[32,64,128]{1,2,0:T(8,128)(2,1)S(1)} %fusion.2, bf16[128,128]{1,0:T(8,128)(2,1)S(1)} %copy-done.2), kind=kOutput, calls=%fused_computation.25 | convolution fusion | flops 67633152 | bytes 2129920 | tf_op jit(solution)/shard_map/ijd,dc->ijc/dot_general | solution.py:35
  (21 shorter events, 2.5 us)
Async XLA Ops:
  6.5 1.0 %copy-start = (bf16[32,64,128]{2,1,0:T(8,128)(2,1)S(1)}, bf16[32,64,128]{2,1,0:T(8,128)(2,1)}, u32[]{:S(2)}) copy-start(bf16[32,64,128]{2,1,0:T(8,128)(2,1)} %param.8) | copy-start | bytes 1572868
  6.5 68.3 %all-gather.2.cloned.1.call-start = ((), (), s32[]{:S(2)}) async-start(), calls=%async_computation.3 | async-start | bytes 2621440 | tf_op jit(solution)/shard_map/all_gather | solution.py:50
  27.5 2.1 %copy-start.1 = (bf16[128,128]{1,0:T(8,128)(2,1)S(1)}, bf16[128,128]{1,0:T(8,128)(2,1)}, u32[]{:S(2)}) copy-start(bf16[128,128]{1,0:T(8,128)(2,1)} %param.10) | copy-start | bytes 98308
  27.9 2.0 %copy-start.4 = (bf16[128,128]{1,0:T(8,128)(2,1)S(1)}, bf16[128,128]{1,0:T(8,128)(2,1)}, u32[]{:S(2)}) copy-start(bf16[128,128]{1,0:T(8,128)(2,1)} %param.12) | copy-start | bytes 98308
  77.2 6.2 %copy-start.5 = (bf16[128,128]{1,0:T(8,128)(2,1)S(1)}, bf16[128,128]{1,0:T(8,128)(2,1)}, u32[]{:S(2)}) copy-start(bf16[128,128]{1,0:T(8,128)(2,1)} %param.15) | copy-start | bytes 98308
  79.6 13.4 %all-to-all-start.2 = ((bf16[8,2,16384]{2,1,0:T(2,128)(2,1)}), bf16[8,2,16384]{2,1,0:T(2,128)(2,1)S(1)}, u32[]{:S(2)}, u32[]{:S(2)}) async-start(bf16[8,2,16384]{2,1,0:T(2,128)(2,1)} %reshape.32), calls=%async_computation.2 | async-start | bytes 1048576 | tf_op jit(solution)/shard_map/all_to_all | solution.py:55
  94.5 0.7 copy-start.3
  95.2 0.8 copy-start.2
Sparse Core Ops, SparseCore 0:
  29.7 45.0 all-gather.1
where the time goes:
time: 105 us; the launch traced here: 104 us
  waiting for transfers between devices  38.2 us (36%)
  blocking collectives  26.8 us (26%)
  between operations  13.6 us (13%)
  local copies, waits for them, and re-layouts  13.5 us (13%)
  matrix products  6.96 us (7%)
  starting transfers between devices  3.68 us (4%)
  other arithmetic  1.27 us (1%)
    all_gather x1, waiting for transfers between devices, on_device(): lax.all_gather(left_lines, 'pc', axis=1, tiled=True)  28.9 us
    all_to_all x1, blocking collectives, on_device(): lax.all_to_all(left, 'pr', split_axis=2, concat_axis=0, tiled=True)  14.7 us
    all_to_all x1, blocking collectives, on_device(): lax.all_to_all(right, 'pr', split_axis=2, concat_axis=0, tiled=True)  12.1 us
    all_to_all x1, waiting for transfers between devices, on_device(): mixed = lax.all_to_all(strip, 'pr', split_axis=0, concat_axis=2, tiled=True)  9.25 us
    unnamed x18, local copies, waits for them, and re-layouts  6.59 us
    all_to_all x1, starting transfers between devices, on_device(): mixed = lax.all_to_all(strip, 'pr', split_axis=0, concat_axis=2, tiled=True)  3.67 us
    convert_element_type x2, local copies, waits for them, and re-layouts, make_factors(): return (pair_in, left.astype(jnp.bfloat16), right.astype(jnp.bfloat16))  3.24 us
    dot_general x1, matrix products, on_device(): jnp.einsum('kid,kjd->ijd', lax.all_gather(left_lines, 'pc', axis=1, tiled...  2.35 us
  transfers between devices with their start and end apart: 2, of which 2 were waited for; matrix products, arithmetic and copies ran while one was open for 4% of the time, Pallas kernels for 0%

commit v1 on v0

v1 whole, which is shorter than its diff:
```python
import functools

import jax
import jax.numpy as jnp
from jax import lax
from jax.experimental import pallas as pl
from jax.experimental.pallas import tpu as pltpu
from jax.sharding import PartitionSpec as P

F32, BF16 = jnp.float32, jnp.bfloat16
LANES = 128
VMEM = pl.BlockSpec(memory_space=pltpu.VMEM)


def dot(a, b, over_a, over_b):
    return lax.dot_general(a, b, (((over_a,), (over_b,)), ((), ())), preferred_element_type=F32)


def logistic(v):
    return 0.5 * jnp.tanh(0.5 * v) + 0.5


def factors_kernel(x_ref, lw_ref, lg_ref, rw_ref, rg_ref, out_ref, left_ref, right_ref):
    width = lw_ref.shape[1]
    rows = x_ref.shape[0] // LANES
    weights = jnp.concatenate(
        [w[...].astype(F32).T.astype(BF16) for w in (lw_ref, lg_ref, rw_ref, rg_ref)], axis=0
    )

    def chunk(s, _):
        x = x_ref[pl.ds(pl.multiple_of(s * 2 * LANES, 2 * LANES), 2 * LANES), :]
        y = dot(weights, x, 1, 1)
        left = y[:width] * logistic(y[width : 2 * width])
        right = y[2 * width : 3 * width] * logistic(y[3 * width :])
        for h in range(2):
            at = pl.ds(2 * s + h, width, stride=rows)
            left_ref[at, :] = left[:, h * LANES : (h + 1) * LANES]
            right_ref[at, :] = right[:, h * LANES : (h + 1) * LANES]
        return 0

    lax.fori_loop(0, rows // 2, chunk, 0, unroll=2)
    shape = (out_ref.shape[0],) + out_ref.shape[2:]
    out_ref[:, 0] = left_ref[...].astype(BF16).reshape(shape)
    out_ref[:, 1] = right_ref[...].astype(BF16).reshape(shape)


def lines_of(ref, ch, fold):
    pr, pc = ref.shape[:2]
    width = LANES // fold
    blocks = [jnp.concatenate([ref[p, c, 0, ch] for p in range(pr)], axis=0) for c in range(pc)]
    return [
        jnp.concatenate([b[:, e * width : (e + 1) * width] for b in blocks], axis=1)
        for e in range(fold)
    ]


def product_kernel(fold, scale, left_ref, right_ref, out_ref):
    rows_of, pc, channels, rows = out_ref.shape[:4]
    width = LANES // fold
    for ch in range(channels):
        left = lines_of(left_ref, ch, fold)
        right = lines_of(right_ref, ch, fold)
        mixed = sum(dot(a, b, 0, 0) for a, b in zip(left, right)) * scale
        for p in range(rows_of):
            at = p * rows * fold
            for c in range(pc):
                block = [
                    mixed[at + f * rows : at + (f + 1) * rows, c * width : (c + 1) * width]
                    for f in range(fold)
                ]
                block = block[0] if fold == 1 else jnp.concatenate(block, axis=1)
                out_ref[p, c, ch] = block.astype(BF16)


def pair_kernel(fold, x_ref, mixed_ref, gain_ref, ow_ref, og_ref, out_ref, held_ref):
    depth, rows = mixed_ref.shape[:2]
    width = LANES // fold
    mixed = mixed_ref[...].astype(F32)
    held_ref[...] = mixed.reshape(depth * rows, LANES)
    mean = jnp.sum(mixed, axis=0) * (1.0 / depth)
    centred = mixed - mean[None]
    root = lax.rsqrt(jnp.sum(centred * centred, axis=0) * (1.0 / depth) + 1e-05)
    gain = jnp.broadcast_to(gain_ref[...], (LANES, depth)).T
    weight, gates = ow_ref[...], og_ref[...]
    for s in range(rows):
        v = held_ref[pl.ds(s, depth, stride=rows), :]
        scaled = ((v - mean[s : s + 1]) * root[s : s + 1] * gain).astype(BF16)
        x = jnp.concatenate([x_ref[f * rows + s] for f in range(fold)], axis=0)
        y = dot(scaled, weight, 0, 0) * logistic(dot(x, gates, 1, 0))
        for f in range(fold):
            out_ref[f * rows + s] = y[f * width : (f + 1) * width].astype(BF16)


def on_device(
    pair_array, left_weight, right_weight, left_gate, right_gate, mid_gain, out_weight, out_gate
):
    pr, pc = lax.axis_size("pr"), lax.axis_size("pc")
    n = pr * pc
    lines, ours, depth = pair_array.shape
    mix = left_weight.shape[1]
    count = lines * pr
    fold = max(1, LANES // ours)
    rows = lines * ours // LANES
    channels = mix // n
    factors = pl.pallas_call(
        factors_kernel,
        out_shape=jax.ShapeDtypeStruct((n, 2, channels * rows, LANES), BF16),
        in_specs=[VMEM] * 5,
        out_specs=VMEM,
        scratch_shapes=[pltpu.VMEM((mix * rows, LANES), F32)] * 2,
        compiler_params=pltpu.CompilerParams(vmem_limit_bytes=48 << 20),
        name="factors",
    )(
        pair_array.reshape(lines * ours, depth), left_weight, left_gate, right_weight, right_gate
    )
    factors = lax.all_to_all(factors, ("pr", "pc"), 0, 0, tiled=True)
    factors = factors.reshape(pr, pc, 2, channels, rows, LANES)
    whole = count * count * 4 * channels <= (2 << 20)
    at_once, blocks = (channels, pc) if whole else (1, 1)
    mixed = pl.pallas_call(
        functools.partial(product_kernel, fold, count ** (-0.5)),
        grid=(channels // at_once, pc // blocks),
        out_shape=jax.ShapeDtypeStruct((pr, pc, channels, rows, LANES), BF16),
        in_specs=[
            pl.BlockSpec((pr, blocks, 1, at_once, rows, LANES), lambda h, c: (0, c, 0, h, 0, 0)),
            pl.BlockSpec((pr, pc, 1, at_once, rows, LANES), lambda h, c: (0, 0, 1, h, 0, 0)),
        ],
        out_specs=pl.BlockSpec(
            (pr * blocks // pc, pc, at_once, rows, LANES), lambda h, c: (c, 0, h, 0, 0)
        ),
        compiler_params=pltpu.CompilerParams(vmem_limit_bytes=48 << 20),
        name="product",
    )(factors, factors)
    mixed = mixed.reshape(n, channels * rows, LANES)
    mixed = lax.all_to_all(mixed, ("pr", "pc"), 0, 0, tiled=True)
    return pl.pallas_call(
        functools.partial(pair_kernel, fold),
        out_shape=jax.ShapeDtypeStruct(pair_array.shape, BF16),
        in_specs=[VMEM] * 5,
        out_specs=VMEM,
        scratch_shapes=[pltpu.VMEM((mix * rows, LANES), F32)],
        compiler_params=pltpu.CompilerParams(vmem_limit_bytes=48 << 20),
        name="pair",
    )(pair_array, mixed.reshape(mix, rows, LANES), mid_gain.reshape(1, mix), out_weight, out_gate)


def solution(mesh):
    return jax.shard_map(
        on_device,
        mesh=mesh,
        in_specs=(P("pr", "pc", None), P(), P(), P(), P(), P(), P(), P()),
        out_specs=P("pr", "pc", None),
        check_vma=False,
    )
```

time: 105 us -> 61.5 us (0.59)
  the two profiles are of different devices: /device:TPU:0 before, /device:TPU:1 now
where the time goes in v1:
time: 61.5 us; the launch traced here: 61 us
  blocking collectives  51.4 us (84%)
  Pallas kernels  4.81 us (8%)
  local copies, waits for them, and re-layouts  4.73 us (8%)
    all_to_all x1, blocking collectives, on_device(): factors = lax.all_to_all(factors, ('pr', 'pc'), 0, 0, tiled=True)  33.2 us
    all_to_all x1, blocking collectives, on_device(): mixed = lax.all_to_all(mixed, ('pr', 'pc'), 0, 0, tiled=True)  18.2 us
    unnamed x18, local copies, waits for them, and re-layouts  4.73 us
    pallas_call x1, Pallas kernels, on_device(): pl.pallas_call(factors_kernel, out_shape=jax.ShapeDtypeStruct((n, 2, chan...  1.83 us
    pallas_call x1, Pallas kernels, on_device(): pl.pallas_call(functools.partial(pair_kernel, fold), out_shape=jax.ShapeD...  1.77 us

profile of v1, /device:TPU:1, one launch (start us, length us, event | category | flops | bytes accessed | tf_op | source)
XLA Modules:
  0.0 61.0 jit_solution(7961066485762983648)
XLA Ops:
  0.0 0.0 copy-start
  0.0 1.0 %copy-done = bf16[32,64,128]{2,1,0:T(8,128)(2,1)S(1)} copy-done((bf16[32,64,128]{2,1,0:T(8,128)(2,1)S(1)}, bf16[32,64,128]{2,1,0:T(8,128)(2,1)}, u32[]{:S(2)}) %copy-start) | copy-done | bytes 524312
  1.0 0.0 copy-start.4
  1.0 0.8 %copy-done.4 = bf16[128,128]{1,0:T(8,128)(2,1)S(1)} copy-done((bf16[128,128]{1,0:T(8,128)(2,1)S(1)}, bf16[128,128]{1,0:T(8,128)(2,1)}, u32[]{:S(2)}) %copy-start.4) | copy-done | bytes 32792
  1.8 0.0 copy-start.5
  1.8 0.8 %copy-done.5 = bf16[128,128]{1,0:T(8,128)(2,1)S(1)} copy-done((bf16[128,128]{1,0:T(8,128)(2,1)S(1)}, bf16[128,128]{1,0:T(8,128)(2,1)}, u32[]{:S(2)}) %copy-start.5) | copy-done | bytes 32792
  2.6 0.0 copy-start.6
  2.6 0.8 %copy-done.6 = bf16[128,128]{1,0:T(8,128)(2,1)S(1)} copy-done((bf16[128,128]{1,0:T(8,128)(2,1)S(1)}, bf16[128,128]{1,0:T(8,128)(2,1)}, u32[]{:S(2)}) %copy-start.6) | copy-done | bytes 32792
  3.3 0.0 copy-start.7
  3.3 0.8 %copy-done.7 = bf16[128,128]{1,0:T(8,128)(2,1)S(1)} copy-done((bf16[128,128]{1,0:T(8,128)(2,1)S(1)}, bf16[128,128]{1,0:T(8,128)(2,1)}, u32[]{:S(2)}) %copy-start.7) | copy-done | bytes 32792
  4.1 1.8 %factors.1 = bf16[32,2,64,128]{3,2,1,0:T(8,128)(2,1)S(1)} custom-call(bf16[2048,128]{1,0:T(8,128)(2,1)S(1)} %bitcast.8, bf16[128,128]{1,0:T(8,128)(2,1)S(1)} %copy-done.4, bf16[128,128]{1,0:T(8,128)(2,1)S(1)} %copy-done.5, bf16[128,128]{1,0:T(8,128)(2,1)S(1)} %copy-done.6, bf16[128,128]{1,0:T(8,128)(2,1)S(1)} %copy-done.7), custom_call_target="tpu_custom_call" | custom-call | tf_op jit(solution)/shard_map/factors/pallas_call | solution.py:105
  5.9 33.2 %all_to_all.10 = bf16[32,2,64,128]{3,2,1,0:T(8,128)(2,1)S(1)} all-to-all(bf16[32,2,64,128]{3,2,1,0:T(8,128)(2,1)S(1)} %factors.1), channel_id=1, replica_groups=mesh['pr'=8,'pc'=4] {'pr','pc'}, dimensions={0} | all-to-all | bytes 2097152 | tf_op jit(solution)/shard_map/all_to_all | solution.py:116
  39.1 1.2 %product.1 = bf16[8,4,4,16,128]{4,3,2,1,0:T(8,128)(2,1)S(1)} custom-call(bf16[8,4,2,4,16,128]{5,4,3,2,1,0:T(8,128)(2,1)S(1)} %bitcast.5, bf16[8,4,2,4,16,128]{5,4,3,2,1,0:T(8,128)(2,1)S(1)} %bitcast.6), custom_call_target="tpu_custom_call" | custom-call | tf_op jit(solution)/shard_map/product/pallas_call | solution.py:120
  40.3 0.0 copy-start.1
  40.4 0.0 copy-start.2
  40.4 0.0 copy-start.3
  40.4 18.2 %all_to_all.11 = bf16[32,64,128]{2,1,0:T(8,128)(2,1)S(1)} all-to-all(bf16[32,64,128]{2,1,0:T(8,128)(2,1)S(1)} %bitcast.7), channel_id=1, replica_groups=mesh['pr'=8,'pc'=4] {'pr','pc'}, dimensions={0} | all-to-all | bytes 1048576 | tf_op jit(solution)/shard_map/all_to_all | solution.py:135
  58.6 0.0 copy-start.8
  58.6 0.0 copy-done.1
  58.6 0.0 copy-done.2
  58.6 0.0 copy-done.3
  58.6 0.6 %copy-done.8 = f32[128]{0:T(128)S(1)} copy-done((f32[128]{0:T(128)S(1)}, f32[128]{0:T(128)}, u32[]{:S(2)}) %copy-start.8) | copy-done | bytes 536
  59.3 1.8 %pair.1 = bf16[32,64,128]{2,1,0:T(8,128)(2,1)} custom-call(bf16[32,64,128]{2,1,0:T(8,128)(2,1)S(1)} %copy-done.1, bf16[128,16,128]{2,1,0:T(8,128)(2,1)S(1)} %bitcast.9, f32[1,128]{1,0:T(1,128)S(1)} %bitcast.10, bf16[128,128]{1,0:T(8,128)(2,1)S(1)} %copy-done.2, bf16[128,128]{1,0:T(8,128)(2,1)S(1)} %copy-done.3), custom_call_target="tpu_custom_call" | custom-call | tf_op jit(solution)/shard_map/pair/pallas_call | solution.py:136
Async XLA Ops:
  0.0 1.0 %copy-start = (bf16[32,64,128]{2,1,0:T(8,128)(2,1)S(1)}, bf16[32,64,128]{2,1,0:T(8,128)(2,1)}, u32[]{:S(2)}) copy-start(bf16[32,64,128]{2,1,0:T(8,128)(2,1)} %x_ref.1) | copy-start | bytes 1572868
  1.0 0.8 %copy-start.4 = (bf16[128,128]{1,0:T(8,128)(2,1)S(1)}, bf16[128,128]{1,0:T(8,128)(2,1)}, u32[]{:S(2)}) copy-start(bf16[128,128]{1,0:T(8,128)(2,1)} %lw_ref.1) | copy-start | bytes 98308
  1.8 0.8 %copy-start.5 = (bf16[128,128]{1,0:T(8,128)(2,1)S(1)}, bf16[128,128]{1,0:T(8,128)(2,1)}, u32[]{:S(2)}) copy-start(bf16[128,128]{1,0:T(8,128)(2,1)} %lg_ref.1) | copy-start | bytes 98308
  2.6 0.8 %copy-start.6 = (bf16[128,128]{1,0:T(8,128)(2,1)S(1)}, bf16[128,128]{1,0:T(8,128)(2,1)}, u32[]{:S(2)}) copy-start(bf16[128,128]{1,0:T(8,128)(2,1)} %rw_ref.1) | copy-start | bytes 98308
  3.3 0.8 %copy-start.7 = (bf16[128,128]{1,0:T(8,128)(2,1)S(1)}, bf16[128,128]{1,0:T(8,128)(2,1)}, u32[]{:S(2)}) copy-start(bf16[128,128]{1,0:T(8,128)(2,1)} %rg_ref.1) | copy-start | bytes 98308
  40.3 18.3 %copy-start.1 = (bf16[32,64,128]{2,1,0:T(8,128)(2,1)S(1)}, bf16[32,64,128]{2,1,0:T(8,128)(2,1)}, u32[]{:S(2)}) copy-start(bf16[32,64,128]{2,1,0:T(8,128)(2,1)} %x_ref.1) | copy-start | bytes 1572868
  40.4 18.3 %copy-start.2 = (bf16[128,128]{1,0:T(8,128)(2,1)S(1)}, bf16[128,128]{1,0:T(8,128)(2,1)}, u32[]{:S(2)}) copy-start(bf16[128,128]{1,0:T(8,128)(2,1)} %ow_ref.1) | copy-start | bytes 98308
  40.4 18.2 %copy-start.3 = (bf16[128,128]{1,0:T(8,128)(2,1)S(1)}, bf16[128,128]{1,0:T(8,128)(2,1)}, u32[]{:S(2)}) copy-start(bf16[128,128]{1,0:T(8,128)(2,1)} %og_ref.1) | copy-start | bytes 98308
  58.6 0.7 %copy-start.8 = (f32[128]{0:T(128)S(1)}, f32[128]{0:T(128)}, u32[]{:S(2)}) copy-start(f32[128]{0:T(128)} %param.13) | copy-start | bytes 1540
